TPU v7x, 32 devices: a whole 2x2x4 slice. The times are simulated.
32 devices in a mesh: groups: 2 (over y), dom: 8 (over z, core), tilt: 2 (over x), rep: 1.
Axes of the slice: x: 2, y: 2, z: 4, core: 2. Of those that a mesh axis runs over, the one named last changes fastest.
Arguments:
- patches: bfloat16 [4, 1024, 128, 128], P(('groups', 'tilt'), 'dom'), parts along dimension 0, may hold values from -6 to 6
- slot_view: int32 [4, 1024, 1], P(('groups', 'tilt'), 'dom'), parts along dimension 0, may hold values from 0 to 31, as said below
- slot_tilt: int32 [4, 1024], P(('groups', 'tilt'), 'dom'), parts along dimension 0, may hold values from 0 to 9
- slot_pos: bfloat16 [2, 4, 1024], P(None, ('groups', 'tilt'), 'dom'), parts along dimension 1, may hold values from 0 to 1
- defocus: bfloat16 [4, 1024], P(('groups', 'tilt'), 'dom'), parts along dimension 0, may hold values from 1 to 3
- projections: bfloat16 [64, 20, 2, 128, 128], P(('groups', 'dom'), 'tilt', None, 'rep'), parts along dimension 0, may hold values from -6 to 6
- warp_grid: float32 [40, 2, 256], P(('groups', 'tilt')), parts along dimension 0, may hold values from -6 to 6
Outputs:
- slot_terms: float32 [3, 4, 1024], P(None, ('groups', 'tilt'), 'dom'), parts along dimension 1
- new_warp: float32 [40, 2, 256], P(('groups', 'tilt')), parts along dimension 0
There are 2 independent parts, one for each index of `groups`. A program takes and returns all parts, laid end to end along the dimension named above; each array names one. Nothing has to cross between parts.
Inputs may be any that keep to these rules, and one draw needn't show every extreme that they name: `slot_view`: view v is owned by dom index v // 4. Among the 128 slots of one device (one tilt index and one dom index) at most 24 name views of any one owner, and in every such block some owner is named exactly 24 times.
All inputs are finite; a program needn't handle non-finite values.
Results may differ from a plain program's by a relative error of at most 0.0018.
Values may be sent and summed in bfloat16 or wider, within the bound.
A program may use at most 64 MiB of HBM per device.

v0:
```python
import math
import jax
import jax.numpy as jnp
from jax import lax
from jax.sharding import PartitionSpec as P

GRID = 16
AMPLITUDE = 0.07
TRUST_FLOOR = 0.02


def signed_freq(index, pixels):
    return jnp.where(index < pixels // 2, index, index - pixels).astype(jnp.float32)


def dft_tables(freq_rows, pixels):
    columns = jnp.arange(pixels, dtype=jnp.int32)
    table_scale = 1.0 / math.sqrt(pixels)
    turns_rows = (freq_rows[:, None] * columns[None, :] % pixels).astype(jnp.float32) * (
        2.0 * math.pi / pixels
    )
    turns_full = (columns[:, None] * columns[None, :] % pixels).astype(jnp.float32) * (
        2.0 * math.pi / pixels
    )
    row_table = jnp.concatenate([jnp.cos(turns_rows), jnp.sin(turns_rows)], axis=0) * table_scale
    col_table = jnp.concatenate([jnp.cos(turns_full), jnp.sin(turns_full)], axis=1) * table_scale
    return (row_table.astype(jnp.bfloat16), col_table.astype(jnp.bfloat16))


def node_weights(pos_x, pos_y, grid_side):
    knot_pos = jnp.arange(grid_side, dtype=jnp.int32).astype(jnp.float32)
    weight_x = jnp.maximum(0.0, 1.0 - jnp.abs(pos_x[:, None] * (grid_side - 1) - knot_pos[None, :]))
    weight_y = jnp.maximum(0.0, 1.0 - jnp.abs(pos_y[:, None] * (grid_side - 1) - knot_pos[None, :]))
    return (weight_y[:, :, None] * weight_x[:, None, :]).reshape(
        pos_x.shape[0], grid_side * grid_side
    )


def spectral_terms(spectrum, ref_blk, focus_blk, shift_blk, freq_rows, pixels):
    row_total = freq_rows.shape[0]
    v_one_cos = spectrum[:, :row_total, :pixels]
    v_one_sin = spectrum[:, :row_total, pixels:]
    v_two_cos = spectrum[:, row_total:, :pixels]
    v_two_sin = spectrum[:, row_total:, pixels:]
    real_part = v_one_cos - v_two_sin
    imag_part = -(v_one_sin + v_two_cos)
    freq_y = signed_freq(freq_rows, pixels)[None, :, None]
    freq_x = signed_freq(jnp.arange(pixels, dtype=jnp.int32), pixels)[None, None, :]
    nyquist = pixels / 2.0
    radius = (freq_y * freq_y + freq_x * freq_x) / (nyquist * nyquist)
    aberration = math.pi * focus_blk[:, None, None] * radius
    contrast = -(
        math.sqrt(1.0 - AMPLITUDE * AMPLITUDE) * jnp.sin(aberration)
        + AMPLITUDE * jnp.cos(aberration)
    )
    phase_angle = (
        2.0
        * math.pi
        / pixels
        * (freq_x * shift_blk[:, 0, None, None] + freq_y * shift_blk[:, 1, None, None])
    )
    cosine = jnp.cos(phase_angle)
    sine_part = jnp.sin(phase_angle)
    ref_real = ref_blk[:, 0].astype(jnp.float32)
    ref_imag = ref_blk[:, 1].astype(jnp.float32)
    model_real = contrast * (ref_real * cosine + ref_imag * sine_part)
    model_imag = contrast * (ref_imag * cosine - ref_real * sine_part)
    diff_real = real_part - model_real
    diff_imag = imag_part - model_imag
    inverse_area = 1.0 / (pixels * pixels)
    energy = jnp.sum(diff_real * diff_real + diff_imag * diff_imag, axis=(1, 2)) * inverse_area
    cross_term = diff_imag * model_real - diff_real * model_imag
    grad_x = 2.0 * inverse_area * jnp.sum(2.0 * math.pi / pixels * freq_x * cross_term, axis=(1, 2))
    grad_y = 2.0 * inverse_area * jnp.sum(2.0 * math.pi / pixels * freq_y * cross_term, axis=(1, 2))
    return jnp.stack([energy, grad_x, grad_y], axis=1)


def on_device(patches, slot_view, slot_tilt, slot_pos, defocus, projections, warp_grid):
    owners = lax.axis_size("dom")
    slot_count = patches.shape[1]
    pixels = patches.shape[-1]
    view_dev = projections.shape[0]
    tilt_dev = warp_grid.shape[0]
    node_count = warp_grid.shape[2]
    capacity = 3 * slot_count // (2 * owners)
    buffer_len = owners * capacity
    chosen_view = slot_view[0, :, 0]
    owner_of = chosen_view // view_dev
    owner_hits = (owner_of[:, None] == jnp.arange(owners, dtype=jnp.int32)[None, :]).astype(
        jnp.int32
    )
    earlier = jnp.cumsum(owner_hits, axis=0) - owner_hits
    slot_rank = jnp.sum(earlier * owner_hits, axis=1)
    target = owner_of * capacity + slot_rank
    matches = target[None, :] == jnp.arange(buffer_len, dtype=jnp.int32)[:, None]
    source = jnp.sum(
        jnp.where(matches, jnp.arange(slot_count, dtype=jnp.int32)[None, :], 0), axis=1
    )
    filled = jnp.any(matches, axis=1)
    patch_rows = jnp.where(filled[:, None, None], patches[0][source], jnp.zeros((), jnp.bfloat16))
    slot_meta = jnp.stack(
        [
            slot_tilt[0].astype(jnp.float32),
            (chosen_view % view_dev).astype(jnp.float32),
            defocus[0].astype(jnp.float32),
            slot_pos[0, 0].astype(jnp.float32),
            slot_pos[1, 0].astype(jnp.float32),
            jnp.ones((slot_count,), jnp.float32),
        ],
        axis=1,
    )
    meta_rows = jnp.where(filled[:, None], slot_meta[source], 0.0).astype(jnp.bfloat16)
    patch_buffer = patch_rows.reshape(owners, capacity, pixels, pixels)
    meta_buffer = meta_rows.reshape(owners, capacity, 6)
    row_span = projections.shape[3]
    freq_rows = lax.axis_index("rep") * row_span + jnp.arange(row_span, dtype=jnp.int32)
    row_table, col_table = dft_tables(freq_rows, pixels)
    row_total = freq_rows.shape[0]
    projected_flat = projections.reshape(view_dev * tilt_dev, 2, row_total, pixels)
    tilt_iota = jnp.arange(tilt_dev, dtype=jnp.int32)
    view_iota = jnp.arange(view_dev, dtype=jnp.int32)

    def one_block(inputs):
        patch_blk, index_blk, focus_blk, shift_blk = inputs
        ref_blk = projected_flat[index_blk]
        first_pass = jnp.einsum(
            "fy,byx->bfx", row_table, patch_blk, preferred_element_type=jnp.float32
        ).astype(jnp.bfloat16)
        spectrum = jnp.einsum(
            "bfx,xk->bfk", first_pass, col_table, preferred_element_type=jnp.float32
        )
        return spectral_terms(spectrum, ref_blk, focus_blk, shift_blk, freq_rows, pixels)

    patch_in = lax.all_to_all(patch_buffer, "dom", split_axis=0, concat_axis=0, tiled=True)
    meta_in = lax.all_to_all(meta_buffer, "dom", split_axis=0, concat_axis=0, tiled=True)
    senders = patch_in.shape[0]
    per_sender = patch_in.shape[1]
    slot_total = senders * per_sender
    meta_flat = meta_in.reshape(slot_total, 6).astype(jnp.float32)
    tilt_match = meta_flat[:, 0:1] == tilt_iota.astype(jnp.float32)[None, :]
    view_match = meta_flat[:, 1:2] == view_iota.astype(jnp.float32)[None, :]
    tilt_local = jnp.sum(jnp.where(tilt_match, tilt_iota[None, :], 0), axis=1)
    view_local = jnp.sum(jnp.where(view_match, view_iota[None, :], 0), axis=1)
    weights = node_weights(meta_flat[:, 3], meta_flat[:, 4], GRID)
    shifts = jnp.sum(warp_grid[tilt_local] * weights[:, None, :], axis=2)
    block_len = math.gcd(slot_total, 16)
    block_count = slot_total // block_len
    per_slot = lax.map(
        one_block,
        (
            patch_in.reshape(block_count, block_len, pixels, pixels),
            (view_local * tilt_dev + tilt_local).reshape(block_count, block_len),
            meta_flat[:, 2].reshape(block_count, block_len),
            shifts.reshape(block_count, block_len, 2),
        ),
    ).reshape(slot_total, 3)
    node_coef = (
        tilt_match.astype(jnp.float32)[:, :, None]
        * per_slot[:, None, 1:3]
        * meta_flat[:, 5, None, None]
    ).reshape(senders, per_sender, 2 * tilt_dev)
    returned = lax.all_to_all(
        per_slot.reshape(senders, per_sender, 3), "dom", split_axis=0, concat_axis=0, tiled=True
    )
    weight_all = weights.reshape(senders, per_sender, node_count)
    own_terms = returned.reshape(buffer_len, 3)[target]
    summed = lax.psum(own_terms, "rep")
    slot_terms = summed.T[:, None, :]
    gradient = jnp.dot(
        node_coef.reshape(-1, 2 * tilt_dev).T,
        weight_all.reshape(-1, node_count),
        precision=lax.Precision.HIGHEST,
        preferred_element_type=jnp.float32,
    ).reshape(tilt_dev, 2, node_count)
    whole_grad = lax.psum(gradient, ("dom", "rep"))
    new_warp = warp_grid - whole_grad / jnp.sqrt(
        whole_grad * whole_grad + TRUST_FLOOR * TRUST_FLOOR
    )
    return (slot_terms, new_warp)


def solution(mesh):
    in_specs = (
        P(("groups", "tilt"), "dom", None, None),
        P(("groups", "tilt"), "dom", None),
        P(("groups", "tilt"), "dom"),
        P(None, ("groups", "tilt"), "dom"),
        P(("groups", "tilt"), "dom"),
        P(("groups", "dom"), "tilt", None, "rep", None),
        P(("groups", "tilt"), None, None),
    )
    out_specs = (P(None, ("groups", "tilt"), "dom"), P(("groups", "tilt"), None, None))
    return jax.shard_map(
        on_device, mesh=mesh, in_specs=in_specs, out_specs=out_specs, check_vma=False
    )
```

profile of v0, /device:TPU:0, one launch (start us, length us, event | category | flops | bytes accessed | tf_op | source)
XLA Modules:
  0.0 444.6 jit_solution(1007006649997248516)
XLA Ops:
  0.6 0.7 and_select_fusion.2
  1.7 0.7 fusion.48
  2.4 0.7 multiply_add_fusion.1
  3.3 0.7 bitcast_convert_fusion
  4.1 0.7 convert_bitcast_fusion
  4.7 0.7 stack.8
  5.6 0.8 gather_fusion.2
  6.5 0.6 select_convert_fusion
  7.2 6.4 %all-to-all-start.1 = ((bf16[8,24,6]{1,2,0:T(8,128)(2,1)}), bf16[8,24,6]{1,2,0:T(8,128)(2,1)S(1)}, u32[]{:S(2)}, u32[]{:S(2)}) async-start(bf16[8,24,6]{1,2,0:T(8,128)(2,1)} %select_convert_fusion), calls=%async_computation.1 | async-start | bytes 32768 | tf_op jit(solution)/shard_map/all_to_all | solution.py:135
  13.5 10.2 %gather_fusion.1 = bf16[192,128,128]{2,1,0:T(8,128)(2,1)} fusion(bf16[128,128,128]{2,1,0:T(8,128)(2,1)} %bitcast.181, s32[1024]{0:T(1024)S(1)} %pad_clamp_fusion.3), kind=kCustom, calls=%fused_computation.1 | custom fusion | bytes 12583680 | tf_op jit(solution)/shard_map/gather | solution.py:100
  23.8 8.6 %copy.103 = bf16[8,24,128,128]{2,3,1,0:T(8,128)(2,1)} copy(bf16[8,24,128,128]{3,2,1,0:T(8,128)(2,1)} %bitcast.179) | data formatting | bytes 12582912 | tf_op jit(solution)/shard_map/gather | solution.py:100
  32.4 5.9 %broadcast_select_fusion = bf16[8,24,128,128]{2,3,1,0:T(8,128)(2,1)} fusion(bf16[8,24,128,128]{2,3,1,0:T(8,128)(2,1)} %copy.103, pred[8,24]{1,0:T(8,128)(4,1)S(1)} %broadcast_in_dim.106), kind=kLoop, calls=%fused_computation.65 | loop fusion | flops 3145728 | bytes 12583104 | tf_op jit(solution)/shard_map/jit(_where)/select_n | solution.py:100
  38.3 5.2 %all-to-all-start = ((bf16[8,24,128,128]{2,3,1,0:T(8,128)(2,1)}), bf16[8,24,128,128]{2,3,1,0:T(8,128)(2,1)}, u32[]{:S(2)}, u32[]{:S(2)}) async-start(bf16[8,24,128,128]{2,3,1,0:T(8,128)(2,1)} %broadcast_select_fusion), calls=%async_computation | async-start | bytes 12582912 | tf_op jit(solution)/shard_map/all_to_all | solution.py:134
  44.4 1.1 gather_fusion.3
  46.3 136.3 %all-to-all-done = bf16[8,24,128,128]{2,3,1,0:T(8,128)(2,1)} async-done(((bf16[8,24,128,128]{2,3,1,0:T(8,128)(2,1)}), bf16[8,24,128,128]{2,3,1,0:T(8,128)(2,1)}, u32[]{:S(2)}, u32[]{:S(2)}) %all-to-all-start) | async-done | bytes 6291488 | tf_op jit(solution)/shard_map/all_to_all | solution.py:134
  182.6 223.7 %while.15 = (s32[]{:T(128)}, f32[12,16,3]{1,0,2:T(8,128)S(1)}, bf16[12,16,128,128]{2,3,1,0:T(8,128)(2,1)}, bf16[256,128]{1,0:T(8,128)(2,1)S(1)}, bf16[128,256]{1...) while((s32[]{:T(128)}, f32[12,16,3]{1,0,2:T(8,128)S(1)}, ...), condition=%wide.region_11.12_spmd.clone.clone, body=%wide.region_7.11_spmd.clone.clone.sunk | while | flops 411868064 | bytes 14461309 | solution.py:148
  182.7 4.5 %fusion.62 = f32[16,256,256]{2,1,0:T(8,128)} fusion(bf16[12,16,128,128]{2,3,1,0:T(8,128)(2,1)} %get-tuple-element.403, s32[]{:T(128)} %get-tuple-element.390, bf16[128,256]{1,0:T(8,128)(2,1)S(1)} %get-tuple-element.405, bf16[256,128]{1,0:T(8,128)(2,1)S(1)} %get-tuple-element.404), kind=kOutput, calls=%fused_computation.10.clone.1 | convolution fusion | flops 403177472 | bytes 4850176 | tf_op jit(solution)/shard_map/while/body/eval_jaxpr/bfx,xk->bfk/dot_general | solution.py:129
  187.2 2.5 gather_fusion
  189.8 10.9 %add_reduce_fusion.2 = (f32[16]{0:T(128)S(1)}, f32[16,128,128]{2,1,0:T(8,128)S(1)}) fusion(f32[16,256,256]{2,1,0:T(8,128)} %fusion.62, bf16[16,2,128,128]{3,2,1,0:T(8,128)(2,1)S(1)} %gather_fusion, f32[16,128]{1,0:T(8,128)S(1)} %get-tuple-element.371, f32[16,128]{1,0:T(8,128)S(1)} %get-tuple-element.372, f32[128,128]{1,0:T(8,128)S(1)} %add_multiply_fusion.3, ...), kind=kLoop, calls=%fused_computation.31.clone.1 | loop fusion | flops 7602160 | bytes 6373504 | tf_op jit(solution)/shard_map/while/body/eval_jaxpr/reduce_sum | solution.py:71
  200.8 0.3 multiply_reduce_fusion.4
  201.3 4.5 %fusion.62 = f32[16,256,256]{2,1,0:T(8,128)} fusion(bf16[12,16,128,128]{2,3,1,0:T(8,128)(2,1)} %get-tuple-element.403, s32[]{:T(128)} %get-tuple-element.390, bf16[128,256]{1,0:T(8,128)(2,1)S(1)} %get-tuple-element.405, bf16[256,128]{1,0:T(8,128)(2,1)S(1)} %get-tuple-element.404), kind=kOutput, calls=%fused_computation.10.clone.1 | convolution fusion | flops 403177472 | bytes 4850176 | tf_op jit(solution)/shard_map/while/body/eval_jaxpr/bfx,xk->bfk/dot_general | solution.py:129
  205.9 2.5 gather_fusion
  208.5 10.9 %add_reduce_fusion.2 = (f32[16]{0:T(128)S(1)}, f32[16,128,128]{2,1,0:T(8,128)S(1)}) fusion(f32[16,256,256]{2,1,0:T(8,128)} %fusion.62, bf16[16,2,128,128]{3,2,1,0:T(8,128)(2,1)S(1)} %gather_fusion, f32[16,128]{1,0:T(8,128)S(1)} %get-tuple-element.371, f32[16,128]{1,0:T(8,128)S(1)} %get-tuple-element.372, f32[128,128]{1,0:T(8,128)S(1)} %add_multiply_fusion.3, ...), kind=kLoop, calls=%fused_computation.31.clone.1 | loop fusion | flops 7602160 | bytes 6373504 | tf_op jit(solution)/shard_map/while/body/eval_jaxpr/reduce_sum | solution.py:71
  219.4 0.3 multiply_reduce_fusion.4
  220.0 4.5 %fusion.62 = f32[16,256,256]{2,1,0:T(8,128)} fusion(bf16[12,16,128,128]{2,3,1,0:T(8,128)(2,1)} %get-tuple-element.403, s32[]{:T(128)} %get-tuple-element.390, bf16[128,256]{1,0:T(8,128)(2,1)S(1)} %get-tuple-element.405, bf16[256,128]{1,0:T(8,128)(2,1)S(1)} %get-tuple-element.404), kind=kOutput, calls=%fused_computation.10.clone.1 | convolution fusion | flops 403177472 | bytes 4850176 | tf_op jit(solution)/shard_map/while/body/eval_jaxpr/bfx,xk->bfk/dot_general | solution.py:129
  224.5 2.5 gather_fusion
  227.1 10.9 %add_reduce_fusion.2 = (f32[16]{0:T(128)S(1)}, f32[16,128,128]{2,1,0:T(8,128)S(1)}) fusion(f32[16,256,256]{2,1,0:T(8,128)} %fusion.62, bf16[16,2,128,128]{3,2,1,0:T(8,128)(2,1)S(1)} %gather_fusion, f32[16,128]{1,0:T(8,128)S(1)} %get-tuple-element.371, f32[16,128]{1,0:T(8,128)S(1)} %get-tuple-element.372, f32[128,128]{1,0:T(8,128)S(1)} %add_multiply_fusion.3, ...), kind=kLoop, calls=%fused_computation.31.clone.1 | loop fusion | flops 7602160 | bytes 6373504 | tf_op jit(solution)/shard_map/while/body/eval_jaxpr/reduce_sum | solution.py:71
  238.1 0.3 multiply_reduce_fusion.4
  238.6 4.5 %fusion.62 = f32[16,256,256]{2,1,0:T(8,128)} fusion(bf16[12,16,128,128]{2,3,1,0:T(8,128)(2,1)} %get-tuple-element.403, s32[]{:T(128)} %get-tuple-element.390, bf16[128,256]{1,0:T(8,128)(2,1)S(1)} %get-tuple-element.405, bf16[256,128]{1,0:T(8,128)(2,1)S(1)} %get-tuple-element.404), kind=kOutput, calls=%fused_computation.10.clone.1 | convolution fusion | flops 403177472 | bytes 4850176 | tf_op jit(solution)/shard_map/while/body/eval_jaxpr/bfx,xk->bfk/dot_general | solution.py:129
  243.2 2.5 gather_fusion
  245.8 10.9 %add_reduce_fusion.2 = (f32[16]{0:T(128)S(1)}, f32[16,128,128]{2,1,0:T(8,128)S(1)}) fusion(f32[16,256,256]{2,1,0:T(8,128)} %fusion.62, bf16[16,2,128,128]{3,2,1,0:T(8,128)(2,1)S(1)} %gather_fusion, f32[16,128]{1,0:T(8,128)S(1)} %get-tuple-element.371, f32[16,128]{1,0:T(8,128)S(1)} %get-tuple-element.372, f32[128,128]{1,0:T(8,128)S(1)} %add_multiply_fusion.3, ...), kind=kLoop, calls=%fused_computation.31.clone.1 | loop fusion | flops 7602160 | bytes 6373504 | tf_op jit(solution)/shard_map/while/body/eval_jaxpr/reduce_sum | solution.py:71
  256.7 0.3 multiply_reduce_fusion.4
  257.3 4.5 %fusion.62 = f32[16,256,256]{2,1,0:T(8,128)} fusion(bf16[12,16,128,128]{2,3,1,0:T(8,128)(2,1)} %get-tuple-element.403, s32[]{:T(128)} %get-tuple-element.390, bf16[128,256]{1,0:T(8,128)(2,1)S(1)} %get-tuple-element.405, bf16[256,128]{1,0:T(8,128)(2,1)S(1)} %get-tuple-element.404), kind=kOutput, calls=%fused_computation.10.clone.1 | convolution fusion | flops 403177472 | bytes 4850176 | tf_op jit(solution)/shard_map/while/body/eval_jaxpr/bfx,xk->bfk/dot_general | solution.py:129
  261.8 2.5 gather_fusion
  264.4 10.9 %add_reduce_fusion.2 = (f32[16]{0:T(128)S(1)}, f32[16,128,128]{2,1,0:T(8,128)S(1)}) fusion(f32[16,256,256]{2,1,0:T(8,128)} %fusion.62, bf16[16,2,128,128]{3,2,1,0:T(8,128)(2,1)S(1)} %gather_fusion, f32[16,128]{1,0:T(8,128)S(1)} %get-tuple-element.371, f32[16,128]{1,0:T(8,128)S(1)} %get-tuple-element.372, f32[128,128]{1,0:T(8,128)S(1)} %add_multiply_fusion.3, ...), kind=kLoop, calls=%fused_computation.31.clone.1 | loop fusion | flops 7602160 | bytes 6373504 | tf_op jit(solution)/shard_map/while/body/eval_jaxpr/reduce_sum | solution.py:71
  275.9 4.5 %fusion.62 = f32[16,256,256]{2,1,0:T(8,128)} fusion(bf16[12,16,128,128]{2,3,1,0:T(8,128)(2,1)} %get-tuple-element.403, s32[]{:T(128)} %get-tuple-element.390, bf16[128,256]{1,0:T(8,128)(2,1)S(1)} %get-tuple-element.405, bf16[256,128]{1,0:T(8,128)(2,1)S(1)} %get-tuple-element.404), kind=kOutput, calls=%fused_computation.10.clone.1 | convolution fusion | flops 403177472 | bytes 4850176 | tf_op jit(solution)/shard_map/while/body/eval_jaxpr/bfx,xk->bfk/dot_general | solution.py:129
  280.5 2.5 gather_fusion
  283.1 10.9 %add_reduce_fusion.2 = (f32[16]{0:T(128)S(1)}, f32[16,128,128]{2,1,0:T(8,128)S(1)}) fusion(f32[16,256,256]{2,1,0:T(8,128)} %fusion.62, bf16[16,2,128,128]{3,2,1,0:T(8,128)(2,1)S(1)} %gather_fusion, f32[16,128]{1,0:T(8,128)S(1)} %get-tuple-element.371, f32[16,128]{1,0:T(8,128)S(1)} %get-tuple-element.372, f32[128,128]{1,0:T(8,128)S(1)} %add_multiply_fusion.3, ...), kind=kLoop, calls=%fused_computation.31.clone.1 | loop fusion | flops 7602160 | bytes 6373504 | tf_op jit(solution)/shard_map/while/body/eval_jaxpr/reduce_sum | solution.py:71
  294.6 4.5 %fusion.62 = f32[16,256,256]{2,1,0:T(8,128)} fusion(bf16[12,16,128,128]{2,3,1,0:T(8,128)(2,1)} %get-tuple-element.403, s32[]{:T(128)} %get-tuple-element.390, bf16[128,256]{1,0:T(8,128)(2,1)S(1)} %get-tuple-element.405, bf16[256,128]{1,0:T(8,128)(2,1)S(1)} %get-tuple-element.404), kind=kOutput, calls=%fused_computation.10.clone.1 | convolution fusion | flops 403177472 | bytes 4850176 | tf_op jit(solution)/shard_map/while/body/eval_jaxpr/bfx,xk->bfk/dot_general | solution.py:129
  299.1 2.5 gather_fusion
  301.7 10.9 %add_reduce_fusion.2 = (f32[16]{0:T(128)S(1)}, f32[16,128,128]{2,1,0:T(8,128)S(1)}) fusion(f32[16,256,256]{2,1,0:T(8,128)} %fusion.62, bf16[16,2,128,128]{3,2,1,0:T(8,128)(2,1)S(1)} %gather_fusion, f32[16,128]{1,0:T(8,128)S(1)} %get-tuple-element.371, f32[16,128]{1,0:T(8,128)S(1)} %get-tuple-element.372, f32[128,128]{1,0:T(8,128)S(1)} %add_multiply_fusion.3, ...), kind=kLoop, calls=%fused_computation.31.clone.1 | loop fusion | flops 7602160 | bytes 6373504 | tf_op jit(solution)/shard_map/while/body/eval_jaxpr/reduce_sum | solution.py:71
  313.2 4.5 %fusion.62 = f32[16,256,256]{2,1,0:T(8,128)} fusion(bf16[12,16,128,128]{2,3,1,0:T(8,128)(2,1)} %get-tuple-element.403, s32[]{:T(128)} %get-tuple-element.390, bf16[128,256]{1,0:T(8,128)(2,1)S(1)} %get-tuple-element.405, bf16[256,128]{1,0:T(8,128)(2,1)S(1)} %get-tuple-element.404), kind=kOutput, calls=%fused_computation.10.clone.1 | convolution fusion | flops 403177472 | bytes 4850176 | tf_op jit(solution)/shard_map/while/body/eval_jaxpr/bfx,xk->bfk/dot_general | solution.py:129
  317.8 2.5 gather_fusion
  320.4 10.9 %add_reduce_fusion.2 = (f32[16]{0:T(128)S(1)}, f32[16,128,128]{2,1,0:T(8,128)S(1)}) fusion(f32[16,256,256]{2,1,0:T(8,128)} %fusion.62, bf16[16,2,128,128]{3,2,1,0:T(8,128)(2,1)S(1)} %gather_fusion, f32[16,128]{1,0:T(8,128)S(1)} %get-tuple-element.371, f32[16,128]{1,0:T(8,128)S(1)} %get-tuple-element.372, f32[128,128]{1,0:T(8,128)S(1)} %add_multiply_fusion.3, ...), kind=kLoop, calls=%fused_computation.31.clone.1 | loop fusion | flops 7602160 | bytes 6373504 | tf_op jit(solution)/shard_map/while/body/eval_jaxpr/reduce_sum | solution.py:71
  331.9 4.5 %fusion.62 = f32[16,256,256]{2,1,0:T(8,128)} fusion(bf16[12,16,128,128]{2,3,1,0:T(8,128)(2,1)} %get-tuple-element.403, s32[]{:T(128)} %get-tuple-element.390, bf16[128,256]{1,0:T(8,128)(2,1)S(1)} %get-tuple-element.405, bf16[256,128]{1,0:T(8,128)(2,1)S(1)} %get-tuple-element.404), kind=kOutput, calls=%fused_computation.10.clone.1 | convolution fusion | flops 403177472 | bytes 4850176 | tf_op jit(solution)/shard_map/while/body/eval_jaxpr/bfx,xk->bfk/dot_general | solution.py:129
  336.4 2.5 gather_fusion
  339.0 10.9 %add_reduce_fusion.2 = (f32[16]{0:T(128)S(1)}, f32[16,128,128]{2,1,0:T(8,128)S(1)}) fusion(f32[16,256,256]{2,1,0:T(8,128)} %fusion.62, bf16[16,2,128,128]{3,2,1,0:T(8,128)(2,1)S(1)} %gather_fusion, f32[16,128]{1,0:T(8,128)S(1)} %get-tuple-element.371, f32[16,128]{1,0:T(8,128)S(1)} %get-tuple-element.372, f32[128,128]{1,0:T(8,128)S(1)} %add_multiply_fusion.3, ...), kind=kLoop, calls=%fused_computation.31.clone.1 | loop fusion | flops 7602160 | bytes 6373504 | tf_op jit(solution)/shard_map/while/body/eval_jaxpr/reduce_sum | solution.py:71
  350.5 4.5 %fusion.62 = f32[16,256,256]{2,1,0:T(8,128)} fusion(bf16[12,16,128,128]{2,3,1,0:T(8,128)(2,1)} %get-tuple-element.403, s32[]{:T(128)} %get-tuple-element.390, bf16[128,256]{1,0:T(8,128)(2,1)S(1)} %get-tuple-element.405, bf16[256,128]{1,0:T(8,128)(2,1)S(1)} %get-tuple-element.404), kind=kOutput, calls=%fused_computation.10.clone.1 | convolution fusion | flops 403177472 | bytes 4850176 | tf_op jit(solution)/shard_map/while/body/eval_jaxpr/bfx,xk->bfk/dot_general | solution.py:129
  355.1 2.5 gather_fusion
  357.7 10.9 %add_reduce_fusion.2 = (f32[16]{0:T(128)S(1)}, f32[16,128,128]{2,1,0:T(8,128)S(1)}) fusion(f32[16,256,256]{2,1,0:T(8,128)} %fusion.62, bf16[16,2,128,128]{3,2,1,0:T(8,128)(2,1)S(1)} %gather_fusion, f32[16,128]{1,0:T(8,128)S(1)} %get-tuple-element.371, f32[16,128]{1,0:T(8,128)S(1)} %get-tuple-element.372, f32[128,128]{1,0:T(8,128)S(1)} %add_multiply_fusion.3, ...), kind=kLoop, calls=%fused_computation.31.clone.1 | loop fusion | flops 7602160 | bytes 6373504 | tf_op jit(solution)/shard_map/while/body/eval_jaxpr/reduce_sum | solution.py:71
  369.2 4.5 %fusion.62 = f32[16,256,256]{2,1,0:T(8,128)} fusion(bf16[12,16,128,128]{2,3,1,0:T(8,128)(2,1)} %get-tuple-element.403, s32[]{:T(128)} %get-tuple-element.390, bf16[128,256]{1,0:T(8,128)(2,1)S(1)} %get-tuple-element.405, bf16[256,128]{1,0:T(8,128)(2,1)S(1)} %get-tuple-element.404), kind=kOutput, calls=%fused_computation.10.clone.1 | convolution fusion | flops 403177472 | bytes 4850176 | tf_op jit(solution)/shard_map/while/body/eval_jaxpr/bfx,xk->bfk/dot_general | solution.py:129
  373.7 2.5 gather_fusion
  376.3 10.9 %add_reduce_fusion.2 = (f32[16]{0:T(128)S(1)}, f32[16,128,128]{2,1,0:T(8,128)S(1)}) fusion(f32[16,256,256]{2,1,0:T(8,128)} %fusion.62, bf16[16,2,128,128]{3,2,1,0:T(8,128)(2,1)S(1)} %gather_fusion, f32[16,128]{1,0:T(8,128)S(1)} %get-tuple-element.371, f32[16,128]{1,0:T(8,128)S(1)} %get-tuple-element.372, f32[128,128]{1,0:T(8,128)S(1)} %add_multiply_fusion.3, ...), kind=kLoop, calls=%fused_computation.31.clone.1 | loop fusion | flops 7602160 | bytes 6373504 | tf_op jit(solution)/shard_map/while/body/eval_jaxpr/reduce_sum | solution.py:71
  387.8 4.5 %fusion.62 = f32[16,256,256]{2,1,0:T(8,128)} fusion(bf16[12,16,128,128]{2,3,1,0:T(8,128)(2,1)} %get-tuple-element.403, s32[]{:T(128)} %get-tuple-element.390, bf16[128,256]{1,0:T(8,128)(2,1)S(1)} %get-tuple-element.405, bf16[256,128]{1,0:T(8,128)(2,1)S(1)} %get-tuple-element.404), kind=kOutput, calls=%fused_computation.10.clone.1 | convolution fusion | flops 403177472 | bytes 4850176 | tf_op jit(solution)/shard_map/while/body/eval_jaxpr/bfx,xk->bfk/dot_general | solution.py:129
  392.4 2.5 gather_fusion
  395.0 10.9 %add_reduce_fusion.2 = (f32[16]{0:T(128)S(1)}, f32[16,128,128]{2,1,0:T(8,128)S(1)}) fusion(f32[16,256,256]{2,1,0:T(8,128)} %fusion.62, bf16[16,2,128,128]{3,2,1,0:T(8,128)(2,1)S(1)} %gather_fusion, f32[16,128]{1,0:T(8,128)S(1)} %get-tuple-element.371, f32[16,128]{1,0:T(8,128)S(1)} %get-tuple-element.372, f32[128,128]{1,0:T(8,128)S(1)} %add_multiply_fusion.3, ...), kind=kLoop, calls=%fused_computation.31.clone.1 | loop fusion | flops 7602160 | bytes 6373504 | tf_op jit(solution)/shard_map/while/body/eval_jaxpr/reduce_sum | solution.py:71
  406.6 0.3 fusion.42
  406.9 26.7 %psum.6 = f32[10,2,256]{2,0,1:T(8,128)S(1)} all-reduce(f32[10,2,256]{2,0,1:T(8,128)S(1)} %fusion.42), channel_id=1, replica_groups=mesh['groups'=2,'dom'=8,'tilt'=2,'rep'=1] {'dom','rep'}, use_global_device_ids=true, to_apply=%region_12.13 | all-reduce | flops 5120 | bytes 40960 | tf_op jit(solution)/shard_map/psum | solution.py:175
  433.7 0.6 copy.111
  434.3 3.3 all-to-all-start.2
  437.6 0.6 copy.118
  438.3 4.9 %all-to-all-done.2 = f32[8,24,3]{1,2,0:T(4,128)S(1)} async-done(((f32[8,24,3]{1,2,0:T(4,128)}), f32[8,24,3]{1,2,0:T(4,128)S(1)}, u32[]{:S(2)}, u32[]{:S(2)}) %all-to-all-start.2) | async-done | bytes 2336 | tf_op jit(solution)/shard_map/all_to_all | solution.py:162
  443.3 0.6 gather_fusion.4
  444.0 0.6 copy.117
  (235 shorter events, 8.9 us)
Async XLA Ops:
  7.2 31.1 %all-to-all-start.1 = ((bf16[8,24,6]{1,2,0:T(8,128)(2,1)}), bf16[8,24,6]{1,2,0:T(8,128)(2,1)S(1)}, u32[]{:S(2)}, u32[]{:S(2)}) async-start(bf16[8,24,6]{1,2,0:T(8,128)(2,1)} %select_convert_fusion), calls=%async_computation.1 | async-start | bytes 32768 | tf_op jit(solution)/shard_map/all_to_all | solution.py:135
  38.3 6.1 %copy-start = (f32[10,2,256]{2,1,0:T(2,128)S(1)}, f32[10,2,256]{2,1,0:T(2,128)}, u32[]{:S(2)}) copy-start(f32[10,2,256]{2,1,0:T(2,128)} %param.15) | copy-start | bytes 61444
  38.3 144.3 %all-to-all-start = ((bf16[8,24,128,128]{2,3,1,0:T(8,128)(2,1)}), bf16[8,24,128,128]{2,3,1,0:T(8,128)(2,1)}, u32[]{:S(2)}, u32[]{:S(2)}) async-start(bf16[8,24,128,128]{2,3,1,0:T(8,128)(2,1)} %broadcast_select_fusion), calls=%async_computation | async-start | bytes 12582912 | tf_op jit(solution)/shard_map/all_to_all | solution.py:134
  434.3 8.9 %all-to-all-start.2 = ((f32[8,24,3]{1,2,0:T(4,128)}), f32[8,24,3]{1,2,0:T(4,128)S(1)}, u32[]{:S(2)}, u32[]{:S(2)}) async-start(f32[8,24,3]{1,2,0:T(4,128)} %copy.111), calls=%async_computation.2 | async-start | bytes 32768 | tf_op jit(solution)/shard_map/all_to_all | solution.py:162
where the time goes:
time: 447 us; the launch traced here: 445 us
  other arithmetic  149 us (33%)
  waiting for transfers between devices  141 us (32%)
  local copies, waits for them, and re-layouts  56.4 us (13%)
  matrix products  54.4 us (12%)
  blocking collectives  26.7 us (6%)
  starting transfers between devices  14.9 us (3%)
    all_to_all x1, waiting for transfers between devices, on_device(): lax.all_to_all(patch_buffer, 'dom', split_axis=0, concat_axis=0, tiled=True)  136 us
    reduce_sum x12, other arithmetic, spectral_terms(): jnp.sum(diff_real * diff_real + diff_imag * diff_imag, axis=(1, 2))  131 us
    dot_general x12, matrix products, one_block(): jnp.einsum('bfx,xk->bfk', first_pass, col_table, preferred_element_type=j...  54.1 us
    gather x12, local copies, waits for them, and re-layouts, one_block(): ref_blk = projected_flat[index_blk]  29.9 us
    psum x1, blocking collectives, on_device(): whole_grad = lax.psum(gradient, ('dom', 'rep'))  26.7 us
    gather x2, local copies, waits for them, and re-layouts, on_device(): patches[0][source]  18.8 us
  transfers between devices with their start and end apart: 3, of which 2 were waited for; matrix products, arithmetic and copies ran while one was open for 6% of the time, Pallas kernels for 0%

commit v1 on v0

--- a/solution.py
+++ b/solution.py
@@ -172,7 +172,7 @@
         precision=lax.Precision.HIGHEST,
         preferred_element_type=jnp.float32,
     ).reshape(tilt_dev, 2, node_count)
-    whole_grad = lax.psum(gradient, ("dom", "rep"))
+    whole_grad = jnp.sum(lax.all_gather(gradient, ("dom", "rep")), axis=0)
     new_warp = warp_grid - whole_grad / jnp.sqrt(
         whole_grad * whole_grad + TRUST_FLOOR * TRUST_FLOOR
     )

time: 447 us -> 434 us (0.971)
  blocking collectives: 26.7 us -> 14 us
    psum x1 -> x0, blocking collectives: 26.7 us -> none  [on_device(): whole_grad = lax.psum(gradient, ('dom', 'rep'))]
    all_gather x0 -> x1, blocking collectives: none -> 14 us  [on_device(): whole_grad = jnp.sum(lax.all_gather(gradient, ('dom', 'rep')), axis=0)]
where the time goes in v1:
time: 434 us; the launch traced here: 432 us
  other arithmetic  150 us (35%)
  waiting for transfers between devices  141 us (32%)
  local copies, waits for them, and re-layouts  55.8 us (13%)
  matrix products  54.4 us (13%)
  starting transfers between devices  14.9 us (3%)
  blocking collectives  14 us (3%)
    all_to_all x1, waiting for transfers between devices, on_device(): lax.all_to_all(patch_buffer, 'dom', split_axis=0, concat_axis=0, tiled=True)  136 us
    reduce_sum x12, other arithmetic, spectral_terms(): jnp.sum(diff_real * diff_real + diff_imag * diff_imag, axis=(1, 2))  131 us
    dot_general x12, matrix products, one_block(): jnp.einsum('bfx,xk->bfk', first_pass, col_table, preferred_element_type=j...  54.1 us
    gather x12, local copies, waits for them, and re-layouts, one_block(): ref_blk = projected_flat[index_blk]  29.9 us
    gather x2, local copies, waits for them, and re-layouts, on_device(): patches[0][source]  18.8 us
    all_gather x1, blocking collectives, on_device(): whole_grad = jnp.sum(lax.all_gather(gradient, ('dom', 'rep')), axis=0)  14 us
  transfers between devices with their start and end apart: 3, of which 2 were waited for; matrix products, arithmetic and copies ran while one was open for 6% of the time, Pallas kernels for 0%

profile of v1, /device:TPU:0, one launch (start us, length us, event | category | flops | bytes accessed | tf_op | source)
XLA Modules:
  0.0 431.9 jit_solution(754713075372084108)
XLA Ops:
  0.6 0.7 and_select_fusion.2
  1.7 0.7 fusion.48
  2.4 0.7 multiply_add_fusion.1
  3.3 0.7 bitcast_convert_fusion
  4.1 0.7 convert_bitcast_fusion
  4.7 0.7 stack.8
  5.6 0.8 gather_fusion.2
  6.5 0.6 select_convert_fusion
  7.2 6.4 %all-to-all-start.1 = ((bf16[8,24,6]{1,2,0:T(8,128)(2,1)}), bf16[8,24,6]{1,2,0:T(8,128)(2,1)S(1)}, u32[]{:S(2)}, u32[]{:S(2)}) async-start(bf16[8,24,6]{1,2,0:T(8,128)(2,1)} %select_convert_fusion), calls=%async_computation.1 | async-start | bytes 32768 | tf_op jit(solution)/shard_map/all_to_all | solution.py:135
  13.5 10.2 %gather_fusion.1 = bf16[192,128,128]{2,1,0:T(8,128)(2,1)} fusion(bf16[128,128,128]{2,1,0:T(8,128)(2,1)} %bitcast.182, s32[1024]{0:T(1024)S(1)} %pad_clamp_fusion.3), kind=kCustom, calls=%fused_computation.1 | custom fusion | bytes 12583680 | tf_op jit(solution)/shard_map/gather | solution.py:100
  23.8 8.6 %copy.97 = bf16[8,24,128,128]{2,3,1,0:T(8,128)(2,1)} copy(bf16[8,24,128,128]{3,2,1,0:T(8,128)(2,1)} %bitcast.180) | data formatting | bytes 12582912 | tf_op jit(solution)/shard_map/gather | solution.py:100
  32.4 5.9 %broadcast_select_fusion = bf16[8,24,128,128]{2,3,1,0:T(8,128)(2,1)} fusion(bf16[8,24,128,128]{2,3,1,0:T(8,128)(2,1)} %copy.97, pred[8,24]{1,0:T(8,128)(4,1)S(1)} %broadcast_in_dim.106), kind=kLoop, calls=%fused_computation.65 | loop fusion | flops 3145728 | bytes 12583104 | tf_op jit(solution)/shard_map/jit(_where)/select_n | solution.py:100
  38.3 5.2 %all-to-all-start = ((bf16[8,24,128,128]{2,3,1,0:T(8,128)(2,1)}), bf16[8,24,128,128]{2,3,1,0:T(8,128)(2,1)}, u32[]{:S(2)}, u32[]{:S(2)}) async-start(bf16[8,24,128,128]{2,3,1,0:T(8,128)(2,1)} %broadcast_select_fusion), calls=%async_computation | async-start | bytes 12582912 | tf_op jit(solution)/shard_map/all_to_all | solution.py:134
  44.4 1.1 gather_fusion.3
  46.3 136.3 %all-to-all-done = bf16[8,24,128,128]{2,3,1,0:T(8,128)(2,1)} async-done(((bf16[8,24,128,128]{2,3,1,0:T(8,128)(2,1)}), bf16[8,24,128,128]{2,3,1,0:T(8,128)(2,1)}, u32[]{:S(2)}, u32[]{:S(2)}) %all-to-all-start) | async-done | bytes 6291488 | tf_op jit(solution)/shard_map/all_to_all | solution.py:134
  182.6 223.7 %while.15 = (s32[]{:T(128)}, f32[12,16,3]{1,0,2:T(8,128)S(1)}, bf16[12,16,128,128]{2,3,1,0:T(8,128)(2,1)}, bf16[256,128]{1,0:T(8,128)(2,1)S(1)}, bf16[128,256]{1...) while((s32[]{:T(128)}, f32[12,16,3]{1,0,2:T(8,128)S(1)}, ...), condition=%wide.region_11.12_spmd.clone.clone, body=%wide.region_7.11_spmd.clone.clone.sunk | while | flops 411868064 | bytes 14461309 | solution.py:148
  182.7 4.5 %fusion.62 = f32[16,256,256]{2,1,0:T(8,128)} fusion(bf16[12,16,128,128]{2,3,1,0:T(8,128)(2,1)} %get-tuple-element.403, s32[]{:T(128)} %get-tuple-element.390, bf16[128,256]{1,0:T(8,128)(2,1)S(1)} %get-tuple-element.405, bf16[256,128]{1,0:T(8,128)(2,1)S(1)} %get-tuple-element.404), kind=kOutput, calls=%fused_computation.10.clone.1 | convolution fusion | flops 403177472 | bytes 4850176 | tf_op jit(solution)/shard_map/while/body/eval_jaxpr/bfx,xk->bfk/dot_general | solution.py:129
  187.2 2.5 gather_fusion
  189.8 10.9 %add_reduce_fusion.2 = (f32[16]{0:T(128)S(1)}, f32[16,128,128]{2,1,0:T(8,128)S(1)}) fusion(f32[16,256,256]{2,1,0:T(8,128)} %fusion.62, bf16[16,2,128,128]{3,2,1,0:T(8,128)(2,1)S(1)} %gather_fusion, f32[16,128]{1,0:T(8,128)S(1)} %get-tuple-element.371, f32[16,128]{1,0:T(8,128)S(1)} %get-tuple-element.372, f32[128,128]{1,0:T(8,128)S(1)} %add_multiply_fusion.3, ...), kind=kLoop, calls=%fused_computation.31.clone.1 | loop fusion | flops 7602160 | bytes 6373504 | tf_op jit(solution)/shard_map/while/body/eval_jaxpr/reduce_sum | solution.py:71
  200.8 0.3 multiply_reduce_fusion.4
  201.3 4.5 %fusion.62 = f32[16,256,256]{2,1,0:T(8,128)} fusion(bf16[12,16,128,128]{2,3,1,0:T(8,128)(2,1)} %get-tuple-element.403, s32[]{:T(128)} %get-tuple-element.390, bf16[128,256]{1,0:T(8,128)(2,1)S(1)} %get-tuple-element.405, bf16[256,128]{1,0:T(8,128)(2,1)S(1)} %get-tuple-element.404), kind=kOutput, calls=%fused_computation.10.clone.1 | convolution fusion | flops 403177472 | bytes 4850176 | tf_op jit(solution)/shard_map/while/body/eval_jaxpr/bfx,xk->bfk/dot_general | solution.py:129
  205.9 2.5 gather_fusion
  208.5 10.9 %add_reduce_fusion.2 = (f32[16]{0:T(128)S(1)}, f32[16,128,128]{2,1,0:T(8,128)S(1)}) fusion(f32[16,256,256]{2,1,0:T(8,128)} %fusion.62, bf16[16,2,128,128]{3,2,1,0:T(8,128)(2,1)S(1)} %gather_fusion, f32[16,128]{1,0:T(8,128)S(1)} %get-tuple-element.371, f32[16,128]{1,0:T(8,128)S(1)} %get-tuple-element.372, f32[128,128]{1,0:T(8,128)S(1)} %add_multiply_fusion.3, ...), kind=kLoop, calls=%fused_computation.31.clone.1 | loop fusion | flops 7602160 | bytes 6373504 | tf_op jit(solution)/shard_map/while/body/eval_jaxpr/reduce_sum | solution.py:71
  219.4 0.3 multiply_reduce_fusion.4
  220.0 4.5 %fusion.62 = f32[16,256,256]{2,1,0:T(8,128)} fusion(bf16[12,16,128,128]{2,3,1,0:T(8,128)(2,1)} %get-tuple-element.403, s32[]{:T(128)} %get-tuple-element.390, bf16[128,256]{1,0:T(8,128)(2,1)S(1)} %get-tuple-element.405, bf16[256,128]{1,0:T(8,128)(2,1)S(1)} %get-tuple-element.404), kind=kOutput, calls=%fused_computation.10.clone.1 | convolution fusion | flops 403177472 | bytes 4850176 | tf_op jit(solution)/shard_map/while/body/eval_jaxpr/bfx,xk->bfk/dot_general | solution.py:129
  224.5 2.5 gather_fusion
  227.1 10.9 %add_reduce_fusion.2 = (f32[16]{0:T(128)S(1)}, f32[16,128,128]{2,1,0:T(8,128)S(1)}) fusion(f32[16,256,256]{2,1,0:T(8,128)} %fusion.62, bf16[16,2,128,128]{3,2,1,0:T(8,128)(2,1)S(1)} %gather_fusion, f32[16,128]{1,0:T(8,128)S(1)} %get-tuple-element.371, f32[16,128]{1,0:T(8,128)S(1)} %get-tuple-element.372, f32[128,128]{1,0:T(8,128)S(1)} %add_multiply_fusion.3, ...), kind=kLoop, calls=%fused_computation.31.clone.1 | loop fusion | flops 7602160 | bytes 6373504 | tf_op jit(solution)/shard_map/while/body/eval_jaxpr/reduce_sum | solution.py:71
  238.1 0.3 multiply_reduce_fusion.4
  238.6 4.5 %fusion.62 = f32[16,256,256]{2,1,0:T(8,128)} fusion(bf16[12,16,128,128]{2,3,1,0:T(8,128)(2,1)} %get-tuple-element.403, s32[]{:T(128)} %get-tuple-element.390, bf16[128,256]{1,0:T(8,128)(2,1)S(1)} %get-tuple-element.405, bf16[256,128]{1,0:T(8,128)(2,1)S(1)} %get-tuple-element.404), kind=kOutput, calls=%fused_computation.10.clone.1 | convolution fusion | flops 403177472 | bytes 4850176 | tf_op jit(solution)/shard_map/while/body/eval_jaxpr/bfx,xk->bfk/dot_general | solution.py:129
  243.2 2.5 gather_fusion
  245.8 10.9 %add_reduce_fusion.2 = (f32[16]{0:T(128)S(1)}, f32[16,128,128]{2,1,0:T(8,128)S(1)}) fusion(f32[16,256,256]{2,1,0:T(8,128)} %fusion.62, bf16[16,2,128,128]{3,2,1,0:T(8,128)(2,1)S(1)} %gather_fusion, f32[16,128]{1,0:T(8,128)S(1)} %get-tuple-element.371, f32[16,128]{1,0:T(8,128)S(1)} %get-tuple-element.372, f32[128,128]{1,0:T(8,128)S(1)} %add_multiply_fusion.3, ...), kind=kLoop, calls=%fused_computation.31.clone.1 | loop fusion | flops 7602160 | bytes 6373504 | tf_op jit(solution)/shard_map/while/body/eval_jaxpr/reduce_sum | solution.py:71
  256.7 0.3 multiply_reduce_fusion.4
  257.3 4.5 %fusion.62 = f32[16,256,256]{2,1,0:T(8,128)} fusion(bf16[12,16,128,128]{2,3,1,0:T(8,128)(2,1)} %get-tuple-element.403, s32[]{:T(128)} %get-tuple-element.390, bf16[128,256]{1,0:T(8,128)(2,1)S(1)} %get-tuple-element.405, bf16[256,128]{1,0:T(8,128)(2,1)S(1)} %get-tuple-element.404), kind=kOutput, calls=%fused_computation.10.clone.1 | convolution fusion | flops 403177472 | bytes 4850176 | tf_op jit(solution)/shard_map/while/body/eval_jaxpr/bfx,xk->bfk/dot_general | solution.py:129
  261.8 2.5 gather_fusion
  264.4 10.9 %add_reduce_fusion.2 = (f32[16]{0:T(128)S(1)}, f32[16,128,128]{2,1,0:T(8,128)S(1)}) fusion(f32[16,256,256]{2,1,0:T(8,128)} %fusion.62, bf16[16,2,128,128]{3,2,1,0:T(8,128)(2,1)S(1)} %gather_fusion, f32[16,128]{1,0:T(8,128)S(1)} %get-tuple-element.371, f32[16,128]{1,0:T(8,128)S(1)} %get-tuple-element.372, f32[128,128]{1,0:T(8,128)S(1)} %add_multiply_fusion.3, ...), kind=kLoop, calls=%fused_computation.31.clone.1 | loop fusion | flops 7602160 | bytes 6373504 | tf_op jit(solution)/shard_map/while/body/eval_jaxpr/reduce_sum | solution.py:71
  275.9 4.5 %fusion.62 = f32[16,256,256]{2,1,0:T(8,128)} fusion(bf16[12,16,128,128]{2,3,1,0:T(8,128)(2,1)} %get-tuple-element.403, s32[]{:T(128)} %get-tuple-element.390, bf16[128,256]{1,0:T(8,128)(2,1)S(1)} %get-tuple-element.405, bf16[256,128]{1,0:T(8,128)(2,1)S(1)} %get-tuple-element.404), kind=kOutput, calls=%fused_computation.10.clone.1 | convolution fusion | flops 403177472 | bytes 4850176 | tf_op jit(solution)/shard_map/while/body/eval_jaxpr/bfx,xk->bfk/dot_general | solution.py:129
  280.5 2.5 gather_fusion
  283.1 10.9 %add_reduce_fusion.2 = (f32[16]{0:T(128)S(1)}, f32[16,128,128]{2,1,0:T(8,128)S(1)}) fusion(f32[16,256,256]{2,1,0:T(8,128)} %fusion.62, bf16[16,2,128,128]{3,2,1,0:T(8,128)(2,1)S(1)} %gather_fusion, f32[16,128]{1,0:T(8,128)S(1)} %get-tuple-element.371, f32[16,128]{1,0:T(8,128)S(1)} %get-tuple-element.372, f32[128,128]{1,0:T(8,128)S(1)} %add_multiply_fusion.3, ...), kind=kLoop, calls=%fused_computation.31.clone.1 | loop fusion | flops 7602160 | bytes 6373504 | tf_op jit(solution)/shard_map/while/body/eval_jaxpr/reduce_sum | solution.py:71
  294.6 4.5 %fusion.62 = f32[16,256,256]{2,1,0:T(8,128)} fusion(bf16[12,16,128,128]{2,3,1,0:T(8,128)(2,1)} %get-tuple-element.403, s32[]{:T(128)} %get-tuple-element.390, bf16[128,256]{1,0:T(8,128)(2,1)S(1)} %get-tuple-element.405, bf16[256,128]{1,0:T(8,128)(2,1)S(1)} %get-tuple-element.404), kind=kOutput, calls=%fused_computation.10.clone.1 | convolution fusion | flops 403177472 | bytes 4850176 | tf_op jit(solution)/shard_map/while/body/eval_jaxpr/bfx,xk->bfk/dot_general | solution.py:129
  299.1 2.5 gather_fusion
  301.7 10.9 %add_reduce_fusion.2 = (f32[16]{0:T(128)S(1)}, f32[16,128,128]{2,1,0:T(8,128)S(1)}) fusion(f32[16,256,256]{2,1,0:T(8,128)} %fusion.62, bf16[16,2,128,128]{3,2,1,0:T(8,128)(2,1)S(1)} %gather_fusion, f32[16,128]{1,0:T(8,128)S(1)} %get-tuple-element.371, f32[16,128]{1,0:T(8,128)S(1)} %get-tuple-element.372, f32[128,128]{1,0:T(8,128)S(1)} %add_multiply_fusion.3, ...), kind=kLoop, calls=%fused_computation.31.clone.1 | loop fusion | flops 7602160 | bytes 6373504 | tf_op jit(solution)/shard_map/while/body/eval_jaxpr/reduce_sum | solution.py:71
  313.2 4.5 %fusion.62 = f32[16,256,256]{2,1,0:T(8,128)} fusion(bf16[12,16,128,128]{2,3,1,0:T(8,128)(2,1)} %get-tuple-element.403, s32[]{:T(128)} %get-tuple-element.390, bf16[128,256]{1,0:T(8,128)(2,1)S(1)} %get-tuple-element.405, bf16[256,128]{1,0:T(8,128)(2,1)S(1)} %get-tuple-element.404), kind=kOutput, calls=%fused_computation.10.clone.1 | convolution fusion | flops 403177472 | bytes 4850176 | tf_op jit(solution)/shard_map/while/body/eval_jaxpr/bfx,xk->bfk/dot_general | solution.py:129
  317.8 2.5 gather_fusion
  320.4 10.9 %add_reduce_fusion.2 = (f32[16]{0:T(128)S(1)}, f32[16,128,128]{2,1,0:T(8,128)S(1)}) fusion(f32[16,256,256]{2,1,0:T(8,128)} %fusion.62, bf16[16,2,128,128]{3,2,1,0:T(8,128)(2,1)S(1)} %gather_fusion, f32[16,128]{1,0:T(8,128)S(1)} %get-tuple-element.371, f32[16,128]{1,0:T(8,128)S(1)} %get-tuple-element.372, f32[128,128]{1,0:T(8,128)S(1)} %add_multiply_fusion.3, ...), kind=kLoop, calls=%fused_computation.31.clone.1 | loop fusion | flops 7602160 | bytes 6373504 | tf_op jit(solution)/shard_map/while/body/eval_jaxpr/reduce_sum | solution.py:71
  331.9 4.5 %fusion.62 = f32[16,256,256]{2,1,0:T(8,128)} fusion(bf16[12,16,128,128]{2,3,1,0:T(8,128)(2,1)} %get-tuple-element.403, s32[]{:T(128)} %get-tuple-element.390, bf16[128,256]{1,0:T(8,128)(2,1)S(1)} %get-tuple-element.405, bf16[256,128]{1,0:T(8,128)(2,1)S(1)} %get-tuple-element.404), kind=kOutput, calls=%fused_computation.10.clone.1 | convolution fusion | flops 403177472 | bytes 4850176 | tf_op jit(solution)/shard_map/while/body/eval_jaxpr/bfx,xk->bfk/dot_general | solution.py:129
  336.4 2.5 gather_fusion
  339.0 10.9 %add_reduce_fusion.2 = (f32[16]{0:T(128)S(1)}, f32[16,128,128]{2,1,0:T(8,128)S(1)}) fusion(f32[16,256,256]{2,1,0:T(8,128)} %fusion.62, bf16[16,2,128,128]{3,2,1,0:T(8,128)(2,1)S(1)} %gather_fusion, f32[16,128]{1,0:T(8,128)S(1)} %get-tuple-element.371, f32[16,128]{1,0:T(8,128)S(1)} %get-tuple-element.372, f32[128,128]{1,0:T(8,128)S(1)} %add_multiply_fusion.3, ...), kind=kLoop, calls=%fused_computation.31.clone.1 | loop fusion | flops 7602160 | bytes 6373504 | tf_op jit(solution)/shard_map/while/body/eval_jaxpr/reduce_sum | solution.py:71
  350.5 4.5 %fusion.62 = f32[16,256,256]{2,1,0:T(8,128)} fusion(bf16[12,16,128,128]{2,3,1,0:T(8,128)(2,1)} %get-tuple-element.403, s32[]{:T(128)} %get-tuple-element.390, bf16[128,256]{1,0:T(8,128)(2,1)S(1)} %get-tuple-element.405, bf16[256,128]{1,0:T(8,128)(2,1)S(1)} %get-tuple-element.404), kind=kOutput, calls=%fused_computation.10.clone.1 | convolution fusion | flops 403177472 | bytes 4850176 | tf_op jit(solution)/shard_map/while/body/eval_jaxpr/bfx,xk->bfk/dot_general | solution.py:129
  355.1 2.5 gather_fusion
  357.7 10.9 %add_reduce_fusion.2 = (f32[16]{0:T(128)S(1)}, f32[16,128,128]{2,1,0:T(8,128)S(1)}) fusion(f32[16,256,256]{2,1,0:T(8,128)} %fusion.62, bf16[16,2,128,128]{3,2,1,0:T(8,128)(2,1)S(1)} %gather_fusion, f32[16,128]{1,0:T(8,128)S(1)} %get-tuple-element.371, f32[16,128]{1,0:T(8,128)S(1)} %get-tuple-element.372, f32[128,128]{1,0:T(8,128)S(1)} %add_multiply_fusion.3, ...), kind=kLoop, calls=%fused_computation.31.clone.1 | loop fusion | flops 7602160 | bytes 6373504 | tf_op jit(solution)/shard_map/while/body/eval_jaxpr/reduce_sum | solution.py:71
  369.2 4.5 %fusion.62 = f32[16,256,256]{2,1,0:T(8,128)} fusion(bf16[12,16,128,128]{2,3,1,0:T(8,128)(2,1)} %get-tuple-element.403, s32[]{:T(128)} %get-tuple-element.390, bf16[128,256]{1,0:T(8,128)(2,1)S(1)} %get-tuple-element.405, bf16[256,128]{1,0:T(8,128)(2,1)S(1)} %get-tuple-element.404), kind=kOutput, calls=%fused_computation.10.clone.1 | convolution fusion | flops 403177472 | bytes 4850176 | tf_op jit(solution)/shard_map/while/body/eval_jaxpr/bfx,xk->bfk/dot_general | solution.py:129
  373.7 2.5 gather_fusion
  376.3 10.9 %add_reduce_fusion.2 = (f32[16]{0:T(128)S(1)}, f32[16,128,128]{2,1,0:T(8,128)S(1)}) fusion(f32[16,256,256]{2,1,0:T(8,128)} %fusion.62, bf16[16,2,128,128]{3,2,1,0:T(8,128)(2,1)S(1)} %gather_fusion, f32[16,128]{1,0:T(8,128)S(1)} %get-tuple-element.371, f32[16,128]{1,0:T(8,128)S(1)} %get-tuple-element.372, f32[128,128]{1,0:T(8,128)S(1)} %add_multiply_fusion.3, ...), kind=kLoop, calls=%fused_computation.31.clone.1 | loop fusion | flops 7602160 | bytes 6373504 | tf_op jit(solution)/shard_map/while/body/eval_jaxpr/reduce_sum | solution.py:71
  387.8 4.5 %fusion.62 = f32[16,256,256]{2,1,0:T(8,128)} fusion(bf16[12,16,128,128]{2,3,1,0:T(8,128)(2,1)} %get-tuple-element.403, s32[]{:T(128)} %get-tuple-element.390, bf16[128,256]{1,0:T(8,128)(2,1)S(1)} %get-tuple-element.405, bf16[256,128]{1,0:T(8,128)(2,1)S(1)} %get-tuple-element.404), kind=kOutput, calls=%fused_computation.10.clone.1 | convolution fusion | flops 403177472 | bytes 4850176 | tf_op jit(solution)/shard_map/while/body/eval_jaxpr/bfx,xk->bfk/dot_general | solution.py:129
  392.4 2.5 gather_fusion
  395.0 10.9 %add_reduce_fusion.2 = (f32[16]{0:T(128)S(1)}, f32[16,128,128]{2,1,0:T(8,128)S(1)}) fusion(f32[16,256,256]{2,1,0:T(8,128)} %fusion.62, bf16[16,2,128,128]{3,2,1,0:T(8,128)(2,1)S(1)} %gather_fusion, f32[16,128]{1,0:T(8,128)S(1)} %get-tuple-element.371, f32[16,128]{1,0:T(8,128)S(1)} %get-tuple-element.372, f32[128,128]{1,0:T(8,128)S(1)} %add_multiply_fusion.3, ...), kind=kLoop, calls=%fused_computation.31.clone.1 | loop fusion | flops 7602160 | bytes 6373504 | tf_op jit(solution)/shard_map/while/body/eval_jaxpr/reduce_sum | solution.py:71
  406.6 0.3 fusion.42
  407.0 14.0 %all-gather = f32[80,2,256]{2,1,0:T(2,128)S(1)} all-gather(f32[10,2,256]{2,1,0:T(2,128)S(1)} %copy.110), channel_id=2, replica_groups=mesh['groups'=2,'dom'=8,'tilt'=2,'rep'=1] {'dom','rep'}, dimensions={0}, use_global_device_ids=true | all-gather | bytes 184320 | tf_op jit(solution)/shard_map/all_gather | solution.py:175
  421.0 0.6 copy.105
  421.6 3.3 all-to-all-start.2
  425.0 0.6 multiply_subtract_fusion.1
  425.6 4.9 %all-to-all-done.2 = f32[8,24,3]{1,2,0:T(4,128)S(1)} async-done(((f32[8,24,3]{1,2,0:T(4,128)}), f32[8,24,3]{1,2,0:T(4,128)S(1)}, u32[]{:S(2)}, u32[]{:S(2)}) %all-to-all-start.2) | async-done | bytes 2336 | tf_op jit(solution)/shard_map/all_to_all | solution.py:162
  430.6 0.6 gather_fusion.4
  431.3 0.6 copy.111
  (236 shorter events, 9.0 us)
Async XLA Ops:
  7.2 31.1 %all-to-all-start.1 = ((bf16[8,24,6]{1,2,0:T(8,128)(2,1)}), bf16[8,24,6]{1,2,0:T(8,128)(2,1)S(1)}, u32[]{:S(2)}, u32[]{:S(2)}) async-start(bf16[8,24,6]{1,2,0:T(8,128)(2,1)} %select_convert_fusion), calls=%async_computation.1 | async-start | bytes 32768 | tf_op jit(solution)/shard_map/all_to_all | solution.py:135
  38.3 6.1 %copy-start = (f32[10,2,256]{2,1,0:T(2,128)S(1)}, f32[10,2,256]{2,1,0:T(2,128)}, u32[]{:S(2)}) copy-start(f32[10,2,256]{2,1,0:T(2,128)} %param.15) | copy-start | bytes 61444
  38.3 144.3 %all-to-all-start = ((bf16[8,24,128,128]{2,3,1,0:T(8,128)(2,1)}), bf16[8,24,128,128]{2,3,1,0:T(8,128)(2,1)}, u32[]{:S(2)}, u32[]{:S(2)}) async-start(bf16[8,24,128,128]{2,3,1,0:T(8,128)(2,1)} %broadcast_select_fusion), calls=%async_computation | async-start | bytes 12582912 | tf_op jit(solution)/shard_map/all_to_all | solution.py:134
  421.6 8.9 %all-to-all-start.2 = ((f32[8,24,3]{1,2,0:T(4,128)}), f32[8,24,3]{1,2,0:T(4,128)S(1)}, u32[]{:S(2)}, u32[]{:S(2)}) async-start(f32[8,24,3]{1,2,0:T(4,128)} %copy.105), calls=%async_computation.2 | async-start | bytes 32768 | tf_op jit(solution)/shard_map/all_to_all | solution.py:162
